TPU v7x, 512 devices: a whole 4x8x8 slice. The times are simulated.
512 devices in a mesh: ra: 128 (over x_lo, y, z), dec: 4 (over x_hi, core).
Axes of the slice: x: 4 (x_hi: 2, x_lo: 2; x = x_hi * 2 + x_lo), y: 8, z: 8, core: 2. Of those that a mesh axis runs over, the one named last changes fastest.
Arguments:
- exposures: float32 [2, 1280, 49152], P(None, 'dec', 'ra'), may hold values from -6 to 6
- inv_variance: float32 [2, 1280, 49152], P(None, 'dec', 'ra'), may hold values from 0.25 to 4
- pixel_valid: int32 [2, 1280, 49152], P(None, 'dec', 'ra'), may hold values 0 or 1
- correlation: int32 [4, 128, 2], P('dec', 'ra'), may hold values 0 or 1
- pixel_offset: int32 [4, 128, 2, 2], P('dec', 'ra'), may hold values from -3 to 3
- subpixel: float32 [4, 128, 2, 2], P('dec', 'ra'), may hold values from -0.5 to 0.5
- psf_match: bfloat16 [63, 63], replicated, may hold values from -0.09375 to 0.09375
Outputs:
- matched: float32 [768, 32768], P('dec', 'ra')
- weight_map: float32 [768, 32768], P('dec', 'ra')
All inputs are finite; a program needn't handle non-finite values. No bound on the sum of `pixel_valid` or of `correlation` on one device may be relied on, other than what follows from the above.
Results may differ from a plain program's by a relative error of at most 0.007.
Values may be sent and summed in bfloat16 or wider, within the bound.
No kernel may reach another device: no remote copies, remote signals or barrier semaphores. Data moves between devices by JAX's collectives and lax.ppermute only.
A program may use at most 128 MiB of HBM per device.

v0:
```python
import jax
import jax.numpy as jnp
from jax import lax
from jax.experimental import pallas as pl
from jax.experimental.pallas import tpu as pltpu
from jax.sharding import PartitionSpec as P


ROWS = 192
COLS = 256
PROWS = 320
PCOLS = 384
BAND = 96
EXT = 256
HALF = 31
SIDE = 63
LEFT = 64 - HALF
TILES_K = 33
PI = 3.141592653589793
F32 = jnp.float32
BF16 = jnp.bfloat16


def swap_pairs(block, axis, start, wrap):
    count = lax.axis_size(axis)
    lows = [i for i in range(start, count, 2) if wrap or i + 1 < count]
    pairs = [(i, (i + 1) % count) for i in lows]
    return lax.ppermute(block, axis, pairs + [(b, a) for a, b in pairs])


def is_odd(axis):
    return (lax.axis_index(axis) & 1) == 1


def sin_pi(z):
    y = z * PI
    y2 = y * y
    poly = 1.0 / 6227020800.0
    for factorial in (-39916800.0, 362880.0, -5040.0, 120.0, -6.0, 1.0):
        poly = poly * y2 + 1.0 / factorial
    return y * poly


def lanczos_map(offset, fraction, direction):
    lane = lax.broadcasted_iota(jnp.int32, (8, 128), 1)
    signed = jnp.where(lane < 64, lane, lane - 128) * direction
    step = signed + offset
    where_at = step.astype(F32) + fraction
    parity = 1.0 - 2.0 * (step & 1).astype(F32)
    frac = jnp.full((8, 128), fraction, F32)
    third = jnp.abs(where_at) * (1.0 / 3.0)
    folded = jnp.where(third > 0.5, 1.0 - third, third)
    safe = jnp.where(where_at == 0.0, 1.0, where_at)
    first = parity * sin_pi(frac) / (safe * PI)
    second = sin_pi(folded) * 3.0 / (jnp.abs(safe) * PI)
    value = jnp.where(where_at == 0.0, 1.0, first * second)
    value = jnp.where(jnp.abs(where_at) < 3.0, value, 0.0)
    rows = jnp.broadcast_to(value[0:1], (128, 128))
    turned = pltpu.roll(rows, 0, 1, stride=1, stride_axis=0)
    down = lax.broadcasted_iota(jnp.int32, (128, 128), 0)
    across = lax.broadcasted_iota(jnp.int32, (128, 128), 1)
    gap = across - down
    diagonal = jnp.where(jnp.abs(gap) <= 64, turned, 0.0)
    upper = jnp.where(gap < -64, turned, 0.0)
    lower = jnp.where(gap > 64, turned, 0.0)
    return jnp.concatenate(
        [
            jnp.concatenate([diagonal, upper], axis=1),
            jnp.concatenate([lower, diagonal], axis=1),
        ],
        axis=0,
    )


def split(value):
    high = value.astype(BF16)
    return high, (value - high.astype(F32)).astype(BF16)


def dot(a, b):
    return lax.dot_general(a, b, (((1,), (0,)), ((), ())), preferred_element_type=F32)


def warp_kernel(
    off_hbm, sub_hbm, cov_hbm, exp_hbm, inv_hbm, val_hbm,
    own, near, far,
    off, sub, cov, exp, inv, val, small, large,
):
    scalars = [
        pltpu.make_async_copy(source, target, small.at[i])
        for i, (source, target) in enumerate(((off_hbm, off), (sub_hbm, sub), (cov_hbm, cov)))
    ]
    images = [
        [
            pltpu.make_async_copy(source.at[e], target.at[e], large.at[e, i])
            for i, (source, target) in enumerate(((inv_hbm, inv), (val_hbm, val), (exp_hbm, exp)))
        ]
        for e in range(2)
    ]
    for copy in scalars + images[0] + images[1]:
        copy.start()
    for copy in scalars:
        copy.wait()
    maps = [
        [
            split(lanczos_map(off[0, 0, e, axis], sub[0, 0, e, axis], direction))
            for axis, direction in ((0, -1), (1, 1))
        ]
        for e in range(2)
    ]
    first = [[None, None], [None, None]]
    for e in range(2):
        (row_high, row_low), (col_high, col_low) = maps[e]
        for copy in images[e]:
            copy.wait()
        covered = cov[0, 0, e].astype(F32)
        masked = inv[e] * (val[e].astype(F32) * covered)
        planes = (masked * exp[e], masked)
        for n in range(2):
            data = planes[n].astype(BF16)
            half_a = dot(row_high[:160], data[:256]) + dot(row_low[:160], data[:256])
            half_b = dot(row_high[96:], data[64:]) + dot(row_low[96:], data[64:])
            half = jnp.concatenate([half_a, half_b], axis=0).astype(BF16)
            for h in range(2):
                piece = half[:, 128 * h : 128 * h + 256]
                out = dot(piece, col_high) + dot(piece, col_low)
                first[n][h] = out if e == 0 else first[n][h] + out
    lane = lax.broadcasted_iota(jnp.int32, (PROWS, 128), 1)
    odd = is_odd("dec")
    for n in range(2):
        left, right = first[n]
        middle = jnp.where(lane < 64, left[:, 128:], right[:, :128])
        whole = jnp.concatenate([left[:, :128], middle, right[:, 128:]], axis=1)
        own[n] = whole[32 : 32 + EXT]
        top, bottom = whole[:BAND], whole[PROWS - BAND :]
        near[n] = jnp.where(odd, top, bottom).astype(BF16)
        far[n] = jnp.where(odd, bottom, top).astype(BF16)


def dec_sum(own, near, far, odd, n, block):
    cut = pl.ds(128 * block, 128)
    first, second = near[n, :, cut].astype(F32), far[n, :, cut].astype(F32)
    above, below = jnp.where(odd, first, second), jnp.where(odd, second, first)
    return [own[n, 0:96, cut] + above, own[n, 96:160, cut], own[n, 160:256, cut] + below]


def pack(planes):
    lane = lax.broadcasted_iota(jnp.int32, (128, 128), 1)
    groups = [plane[128 * i : 128 * i + 128] for plane in planes for i in range(2)]
    return jnp.concatenate(
        [
            jnp.where(lane < 96, groups[i], pltpu.roll(groups[3], 96 - 32 * i, 1))
            for i in range(3)
        ],
        axis=0,
    )


def unpack(packed):
    lane = lax.broadcasted_iota(jnp.int32, (128, 128), 1)
    groups = [packed[128 * i : 128 * i + 128] for i in range(3)]
    last = pltpu.roll(groups[0], 32, 1)
    last = jnp.where(lane < 32, last, pltpu.roll(groups[1], 64, 1))
    last = jnp.where(lane < 64, last, pltpu.roll(groups[2], 96, 1))
    groups.append(last)
    return [jnp.concatenate(groups[2 * n : 2 * n + 2], axis=0) for n in range(2)]


def edges_kernel(own, near, far, one, two):
    odd = is_odd("dec")
    west = pack([jnp.concatenate(dec_sum(own, near, far, odd, n, 0), axis=0) for n in range(2)])
    east = pack(
        [
            pltpu.roll(jnp.concatenate(dec_sum(own, near, far, odd, n, 2), axis=0), 96, 1)
            for n in range(2)
        ]
    )
    odd = is_odd("ra")
    one[...] = jnp.where(odd, west, east).astype(BF16)
    two[...] = jnp.where(odd, east, west).astype(BF16)


def psf_kernel(psf, weights, taps):
    down = lax.broadcasted_iota(jnp.int32, (SIDE, 128), 0)
    across = lax.broadcasted_iota(jnp.int32, (SIDE, 128), 1)
    reverse = jnp.where(((down + across) & 127) == 0, 1.0, 0.0).astype(BF16)
    taps[...] = jnp.zeros((80, 128), F32)
    taps[8 : 8 + SIDE] = dot(psf[...], reverse)
    lane = lax.broadcasted_iota(jnp.int32, (128, 128), 1)
    weights[0] = jnp.zeros((256, 128), BF16)
    weights[TILES_K] = jnp.zeros((256, 128), BF16)
    for q in range(64):
        here = jnp.broadcast_to(taps[8 + q : 9 + q], (128, 128))
        prev = jnp.broadcast_to(taps[7 + q : 8 + q], (128, 128))
        here = pltpu.roll(here, 0, 1, stride=1, stride_axis=0)
        prev = pltpu.roll(prev, 64, 1, stride=1, stride_axis=0)
        weights[1 + q // 2, 128 * (q % 2) : 128 * (q % 2) + 128] = jnp.where(
            lane < 64, here, prev
        ).astype(BF16)


def match_kernel(own, near, far, one, two, weights, out, weight_map, windows, stage):
    odd = is_odd("ra")
    first, second = one[...].astype(F32), two[...].astype(F32)
    west = [pltpu.roll(plane, 32, 1) for plane in unpack(jnp.where(odd, first, second))]
    east = unpack(jnp.where(odd, second, first))
    lane = lax.broadcasted_iota(jnp.int32, (EXT, 128), 1)
    odd = is_odd("dec")
    numer, denom = [], []
    for n, plane in ((0, numer), (1, denom)):
        for block in range(3):
            whole = jnp.concatenate(dec_sum(own, near, far, odd, n, block), axis=0)
            if block == 0:
                whole = whole + jnp.where(lane >= 32, west[n], 0.0)
            if block == 2:
                whole = whole + jnp.where(lane < 96, east[n], 0.0)
            plane.append(whole)
    denom = jnp.concatenate(denom, axis=1)
    numer = jnp.concatenate(numer, axis=1)
    row = lax.broadcasted_iota(jnp.int32, (EXT, PCOLS), 0) + (lax.axis_index("dec") * ROWS - 32)
    inside = (row >= 0) & (row < lax.axis_size("dec") * ROWS)
    coadd = jnp.where(inside, numer / jnp.maximum(denom, 1.0), 0.0).astype(BF16).astype(F32)
    weight_map[...] = pltpu.roll(denom, PCOLS - 64, 1)[32 : 32 + ROWS, :COLS]
    even = pltpu.roll(coadd, PCOLS - LEFT, 1)
    odd = pltpu.roll(coadd, PCOLS - LEFT - 64, 1)
    for k in range(4):
        source = odd if k % 2 else even
        windows[k, 0:EXT] = source[:, 128 * (k // 2) : 128 * (k // 2) + 128]
    total = None
    for t in range(TILES_K):
        left = jnp.concatenate(
            [
                jnp.concatenate(
                    [windows[k, pl.ds(2 * t + s + 1, 48, stride=4), :] for k in range(4)], axis=0
                )
                for s in range(2)
            ],
            axis=1,
        ).astype(BF16)
        right = jnp.concatenate([weights[t + 1], weights[t]], axis=1)
        part = dot(left, right)
        total = part if total is None else total + part
    lane = lax.broadcasted_iota(jnp.int32, (48, 128), 1)
    for h in range(2):
        lows = total[96 * h : 96 * h + 48]
        highs = total[96 * h + 48 : 96 * h + 96]
        for p in range(4):
            cut = slice(128 * (p // 2), 128 * (p // 2) + 128)
            low, high = lows[:, cut], highs[:, cut]
            if p % 2:
                low = pltpu.roll(low, 64, 1)
            else:
                high = pltpu.roll(high, 64, 1)
            stage[h, pl.ds(p, 48, stride=4), :] = jnp.where(lane < 64, low, high)
        out[:, 128 * h : 128 * h + 128] = stage[h]


HBM = pl.BlockSpec(memory_space=pltpu.HBM)
VMEM = pl.BlockSpec(memory_space=pltpu.VMEM)


def call(body, ins, outs, scratch=(), flops=0, limit=16):
    return pl.pallas_call(
        body,
        in_specs=ins,
        out_specs=tuple(VMEM for _ in outs),
        out_shape=outs,
        scratch_shapes=scratch,
        cost_estimate=pl.CostEstimate(flops=flops, transcendentals=0, bytes_accessed=4_000_000),
        compiler_params=pltpu.CompilerParams(vmem_limit_bytes=limit * 1024 * 1024),
    )


def array(shape, kind):
    return jax.ShapeDtypeStruct(shape, kind)


def shards(exposures, inv_variance, pixel_valid, correlation, pixel_offset, subpixel, psf_match):
    own, near, far = call(
        warp_kernel,
        [HBM] * 6,
        (array((2, EXT, PCOLS), F32), array((2, BAND, PCOLS), BF16), array((2, BAND, PCOLS), BF16)),
        scratch=[
            pltpu.SMEM((1, 1, 2, 2), jnp.int32),
            pltpu.SMEM((1, 1, 2, 2), F32),
            pltpu.SMEM((1, 1, 2), jnp.int32),
            pltpu.VMEM((2, PROWS, PCOLS), F32),
            pltpu.VMEM((2, PROWS, PCOLS), F32),
            pltpu.VMEM((2, PROWS, PCOLS), jnp.int32),
            pltpu.SemaphoreType.DMA((3,)),
            pltpu.SemaphoreType.DMA((2, 3)),
        ],
        flops=3_000_000_000,
    )(
        *(
            pltpu.with_memory_space_constraint(x, pltpu.HBM)
            for x in (pixel_offset, subpixel, correlation, exposures, inv_variance, pixel_valid)
        )
    )
    far = swap_pairs(far, "dec", 1, False)
    near = swap_pairs(near, "dec", 0, False)
    (weights,) = call(
        psf_kernel,
        [VMEM],
        (array((TILES_K + 1, 256, 128), BF16),),
        scratch=[pltpu.VMEM((80, 128), F32)],
        flops=3_000_000_000,
    )(psf_match)
    one, two = call(
        edges_kernel,
        [VMEM] * 3,
        (array((384, 128), BF16), array((384, 128), BF16)),
        flops=1_000_000,
    )(own, near, far)
    one = swap_pairs(one, "ra", 0, True)
    two = swap_pairs(two, "ra", 1, True)
    return call(
        match_kernel,
        [VMEM] * 6,
        (array((ROWS, COLS), F32), array((ROWS, COLS), F32)),
        scratch=[pltpu.VMEM((4, EXT + 8, 128), F32), pltpu.VMEM((2, ROWS, 128), F32)],
        flops=3_000_000_000,
    )(own, near, far, one, two, weights)


def solution(mesh):
    return jax.shard_map(
        shards,
        mesh=mesh,
        in_specs=(
            P(None, "dec", "ra"),
            P(None, "dec", "ra"),
            P(None, "dec", "ra"),
            P("dec", "ra", None),
            P("dec", "ra", None, None),
            P("dec", "ra", None, None),
            P(),
        ),
        out_specs=(P("dec", "ra"), P("dec", "ra")),
        check_vma=False,
    )
```

profile of v0, /device:TPU:1, one launch (start us, length us, event | category | flops | bytes accessed | tf_op | source)
XLA Modules:
  0.0 36.4 jit_solution(12310400684851426119)
XLA Ops:
  0.6 0.0 copy-start
  0.6 3.4 %shard_map.86 = (f32[2,256,384]{2,1,0:T(8,128)S(1)}, bf16[2,96,384]{2,1,0:T(8,128)(2,1)S(1)}, bf16[2,96,384]{2,1,0:T(8,128)(2,1)S(1)}) custom-call(s32[1,1,2,2]{3,2,1,0:T(2,128)} %off_hbm.1, f32[1,1,2,2]{3,2,1,0:T(2,128)} %sub_hbm.1, s32[1,1,2]{2,1,0:T(1,128)} %cov_hbm.1, f32[2,320,384]{2,1,0:T(8,128)} %exp_hbm.1, f32[2,320,384]{2,1,0:T(8,128)} %inv_hbm.1, ...), custom_call_target="tpu_custom_call" | custom-call | flops 3000000000 | bytes 4000000 | tf_op jit(solution)/shard_map/pallas_call | solution.py:279
  4.0 8.7 %collective-permute-start = (bf16[2,96,384]{2,1,0:T(8,128)(2,1)S(1)}, bf16[2,96,384]{2,1,0:T(8,128)(2,1)S(1)}, u32[]{:S(2)}, u32[]{:S(2)}) collective-permute-start(bf16[2,96,384]{2,1,0:T(8,128)(2,1)S(1)} %get-tuple-element.8), channel_id=1, source_target_pairs={{0,1},{2,3},{1,0},{3,2},{4,5},{6,7},{5,4},{7,6},{8,9},{10,11},{9,8... | collective-permute-start | bytes 442376 | tf_op jit(solution)/shard_map/ppermute | solution.py:28
  12.8 1.9 %collective-permute-start.1 = (bf16[2,96,384]{2,1,0:T(8,128)(2,1)S(1)}, bf16[2,96,384]{2,1,0:T(8,128)(2,1)S(1)}, u32[]{:S(2)}, u32[]{:S(2)}) collective-permute-start(bf16[2,96,384]{2,1,0:T(8,128)(2,1)S(1)} %get-tuple-element.9), channel_id=1, source_target_pairs={{1,2},{2,1},{5,6},{6,5},{9,10},{10,9},{13,14},{14,13},{17,18},{18,... | collective-permute-start | bytes 442376 | tf_op jit(solution)/shard_map/ppermute | solution.py:28
  14.7 0.0 collective-permute-done.near
  14.7 6.0 %collective-permute-done.1.far = bf16[2,96,384]{2,1,0:T(8,128)(2,1)S(1)} collective-permute-done((bf16[2,96,384]{2,1,0:T(8,128)(2,1)S(1)}, bf16[2,96,384]{2,1,0:T(8,128)(2,1)S(1)}, u32[]{:S(2)}, u32[]{:S(2)}) %collective-permute-start.1) | collective-permute-done | bytes 147488 | tf_op jit(solution)/shard_map/ppermute | solution.py:28
  20.7 0.2 shard_map.87
  21.0 1.9 %collective-permute-start.2 = (bf16[384,128]{1,0:T(8,128)(2,1)S(1)}, bf16[384,128]{1,0:T(8,128)(2,1)S(1)}, u32[]{:S(2)}, u32[]{:S(2)}) collective-permute-start(bf16[384,128]{1,0:T(8,128)(2,1)S(1)} %get-tuple-element.10), channel_id=1, source_target_pairs={{0,4},{8,12},{16,20},{24,28},{32,36},{40,44},{48,52},{56,60},{64,6... | collective-permute-start | bytes 294920 | tf_op jit(solution)/shard_map/ppermute | solution.py:28
  22.9 9.4 %collective-permute-start.3 = (bf16[384,128]{1,0:T(8,128)(2,1)S(1)}, bf16[384,128]{1,0:T(8,128)(2,1)S(1)}, u32[]{:S(2)}, u32[]{:S(2)}) collective-permute-start(bf16[384,128]{1,0:T(8,128)(2,1)S(1)} %get-tuple-element.11), channel_id=1, source_target_pairs={{4,8},{12,16},{20,24},{28,32},{36,40},{44,48},{52,56},{60,64},{68,... | collective-permute-start | bytes 294920 | tf_op jit(solution)/shard_map/ppermute | solution.py:28
  32.3 0.0 copy-done
  32.3 1.3 %shard_map.88.weights = bf16[34,256,128]{2,1,0:T(8,128)(2,1)S(1)} custom-call(bf16[63,63]{1,0:T(8,128)(2,1)S(1)} %copy-done), custom_call_target="tpu_custom_call" | custom-call | flops 3000000000 | bytes 4000000 | tf_op jit(solution)/shard_map/pallas_call | solution.py:302
  33.6 0.0 collective-permute-done.2.one
  33.6 0.7 %collective-permute-done.3.two = bf16[384,128]{1,0:T(8,128)(2,1)S(1)} collective-permute-done((bf16[384,128]{1,0:T(8,128)(2,1)S(1)}, bf16[384,128]{1,0:T(8,128)(2,1)S(1)}, u32[]{:S(2)}, u32[]{:S(2)}) %collective-permute-start.3) | collective-permute-done | bytes 98336 | tf_op jit(solution)/shard_map/ppermute | solution.py:28
  34.3 2.1 %shard_map.89 = (f32[192,256]{1,0:T(8,128)}, f32[192,256]{1,0:T(8,128)}) custom-call(f32[2,256,384]{2,1,0:T(8,128)S(1)} %get-tuple-element.7.own, bf16[2,96,384]{2,1,0:T(8,128)(2,1)S(1)} %collective-permute-done.near, bf16[2,96,384]{2,1,0:T(8,128)(2,1)S(1)} %collective-permute-done.1.far, bf16[384,128]{1,0:T(8,128)(2,1)S(1)} %collective-permute-done.2.one, ...), custom_call_target="tpu_custom_call" | custom-call | flops 3000000000 | bytes 4000000 | tf_op jit(solution)/shard_map/pallas_call | solution.py:317
Async XLA Ops:
  0.6 31.7 %copy-start = (bf16[63,63]{1,0:T(8,128)(2,1)S(1)}, bf16[63,63]{1,0:T(8,128)(2,1)}, u32[]{:S(2)}) copy-start(bf16[63,63]{1,0:T(8,128)(2,1)} %psf.1) | copy-start | bytes 23818
  4.0 10.7 %collective-permute-start = (bf16[2,96,384]{2,1,0:T(8,128)(2,1)S(1)}, bf16[2,96,384]{2,1,0:T(8,128)(2,1)S(1)}, u32[]{:S(2)}, u32[]{:S(2)}) collective-permute-start(bf16[2,96,384]{2,1,0:T(8,128)(2,1)S(1)} %get-tuple-element.8), channel_id=1, source_target_pairs={{0,1},{2,3},{1,0},{3,2},{4,5},{6,7},{5,4},{7,6},{8,9},{10,11},{9,8... | collective-permute-start | bytes 442376 | tf_op jit(solution)/shard_map/ppermute | solution.py:28
  12.8 8.0 %collective-permute-start.1 = (bf16[2,96,384]{2,1,0:T(8,128)(2,1)S(1)}, bf16[2,96,384]{2,1,0:T(8,128)(2,1)S(1)}, u32[]{:S(2)}, u32[]{:S(2)}) collective-permute-start(bf16[2,96,384]{2,1,0:T(8,128)(2,1)S(1)} %get-tuple-element.9), channel_id=1, source_target_pairs={{1,2},{2,1},{5,6},{6,5},{9,10},{10,9},{13,14},{14,13},{17,18},{18,... | collective-permute-start | bytes 442376 | tf_op jit(solution)/shard_map/ppermute | solution.py:28
  21.0 12.7 %collective-permute-start.2 = (bf16[384,128]{1,0:T(8,128)(2,1)S(1)}, bf16[384,128]{1,0:T(8,128)(2,1)S(1)}, u32[]{:S(2)}, u32[]{:S(2)}) collective-permute-start(bf16[384,128]{1,0:T(8,128)(2,1)S(1)} %get-tuple-element.10), channel_id=1, source_target_pairs={{0,4},{8,12},{16,20},{24,28},{32,36},{40,44},{48,52},{56,60},{64,6... | collective-permute-start | bytes 294920 | tf_op jit(solution)/shard_map/ppermute | solution.py:28
  22.9 11.4 %collective-permute-start.3 = (bf16[384,128]{1,0:T(8,128)(2,1)S(1)}, bf16[384,128]{1,0:T(8,128)(2,1)S(1)}, u32[]{:S(2)}, u32[]{:S(2)}) collective-permute-start(bf16[384,128]{1,0:T(8,128)(2,1)S(1)} %get-tuple-element.11), channel_id=1, source_target_pairs={{4,8},{12,16},{20,24},{28,32},{36,40},{44,48},{52,56},{60,64},{68,... | collective-permute-start | bytes 294920 | tf_op jit(solution)/shard_map/ppermute | solution.py:28
where the time goes:
time: 36.6 us; the launch traced here: 36.4 us
  starting transfers between devices  22 us (60%)
  Pallas kernels  6.98 us (19%)
  waiting for transfers between devices  6.72 us (18%)
  between operations  0.72 us (2%)
    ppermute x4, starting transfers between devices, swap_pairs(): return lax.ppermute(block, axis, pairs + [(b, a) for a, b in pairs])  22 us
    ppermute x4, waiting for transfers between devices, swap_pairs(): return lax.ppermute(block, axis, pairs + [(b, a) for a, b in pairs])  6.72 us
    pallas_call x1, Pallas kernels, shards(): call(warp_kernel, [HBM] * 6, (array((2, EXT, PCOLS), F32), array((2, BAND...  3.35 us
    pallas_call x1, Pallas kernels, shards(): call(match_kernel, [VMEM] * 6, (array((ROWS, COLS), F32), array((ROWS, CO...  2.11 us
    pallas_call x1, Pallas kernels, shards(): call(psf_kernel, [VMEM], (array((TILES_K + 1, 256, 128), BF16),), scratch...  1.28 us
  transfers between devices with their start and end apart: 4, of which 2 were waited for; matrix products, arithmetic and copies ran while one was open for 0% of the time, Pallas kernels for 4%

commit v1 on v0

v1 whole, which is shorter than its diff:
```python
import jax
import jax.numpy as jnp
from jax import lax
from jax.experimental import pallas as pl
from jax.experimental.pallas import tpu as pltpu
from jax.sharding import PartitionSpec as P


ROWS = 192
COLS = 256
PROWS = 320
PCOLS = 384
BAND = 96
EXT = 256
HALF = 31
SIDE = 63
LEFT = 64 - HALF
TILES_K = 33
PI = 3.141592653589793
F32 = jnp.float32
BF16 = jnp.bfloat16


def swap_pairs(block, axis, firsts, wrap):
    count = lax.axis_size(axis)
    lows = [i for i in range(count) if firsts(i) and (wrap or i + 1 < count)]
    if not lows:
        return jnp.zeros_like(block)
    pairs = [(i, (i + 1) % count) for i in lows]
    return lax.ppermute(block, axis, pairs + [(b, a) for a, b in pairs])


def is_odd(axis):
    return (lax.axis_index(axis) & 1) == 1


def sin_pi(z):
    y = z * PI
    y2 = y * y
    poly = 1.0 / 6227020800.0
    for factorial in (-39916800.0, 362880.0, -5040.0, 120.0, -6.0, 1.0):
        poly = poly * y2 + 1.0 / factorial
    return y * poly


def lanczos_map(offset, fraction, direction):
    lane = lax.broadcasted_iota(jnp.int32, (8, 128), 1)
    signed = jnp.where(lane < 64, lane, lane - 128) * direction
    step = signed + offset
    where_at = step.astype(F32) + fraction
    parity = 1.0 - 2.0 * (step & 1).astype(F32)
    frac = jnp.full((8, 128), fraction, F32)
    third = jnp.abs(where_at) * (1.0 / 3.0)
    folded = jnp.where(third > 0.5, 1.0 - third, third)
    safe = jnp.where(where_at == 0.0, 1.0, where_at)
    first = parity * sin_pi(frac) / (safe * PI)
    second = sin_pi(folded) * 3.0 / (jnp.abs(safe) * PI)
    value = jnp.where(where_at == 0.0, 1.0, first * second)
    value = jnp.where(jnp.abs(where_at) < 3.0, value, 0.0)
    rows = jnp.broadcast_to(value[0:1], (128, 128))
    turned = pltpu.roll(rows, 0, 1, stride=1, stride_axis=0)
    down = lax.broadcasted_iota(jnp.int32, (128, 128), 0)
    across = lax.broadcasted_iota(jnp.int32, (128, 128), 1)
    gap = across - down
    diagonal = jnp.where(jnp.abs(gap) <= 64, turned, 0.0)
    upper = jnp.where(gap < -64, turned, 0.0)
    lower = jnp.where(gap > 64, turned, 0.0)
    return diagonal, upper, lower


def row_map(offset, fraction):
    return jnp.concatenate(split(lanczos_map(offset, fraction, -1)[0]), axis=1)


def col_map(offset, fraction):
    diagonal, upper, lower = lanczos_map(offset, fraction, 1)
    return split(
        jnp.concatenate(
            [
                jnp.concatenate([diagonal, upper], axis=1),
                jnp.concatenate([lower, diagonal], axis=1),
            ],
            axis=0,
        )
    )


def split(value):
    high = value.astype(BF16)
    return high, (value - high.astype(F32)).astype(BF16)


def dot(a, b):
    return lax.dot_general(a, b, (((1,), (0,)), ((), ())), preferred_element_type=F32)


def joined(left, right):
    lane = lax.broadcasted_iota(jnp.int32, left[:, :128].shape, 1)
    middle = jnp.where(lane < 64, left[:, 128:], right[:, :128])
    return jnp.concatenate([left[:, :128], middle, right[:, 128:]], axis=1)


def warp_cols(halves, cols):
    planes = []
    for n in range(2):
        sides = []
        for h in range(2):
            at = PCOLS * n + 128 * h
            parts = [
                dot(half[:, at : at + 256], part)
                for half, pair in zip(halves, cols)
                for part in pair
            ]
            sides.append((parts[0] + parts[1]) + (parts[2] + parts[3]))
        planes.append(joined(*sides))
    return planes


def warp_kernel(
    off_hbm, sub_hbm, cov_hbm, exp_hbm, inv_hbm, val_hbm,
    own, near, far, middle, row_maps, col_maps,
    off, sub, cov, exp, inv, val, small, large,
):
    scalars = [
        pltpu.make_async_copy(source, target, small.at[i])
        for i, (source, target) in enumerate(((off_hbm, off), (sub_hbm, sub), (cov_hbm, cov)))
    ]
    images = [
        [
            pltpu.make_async_copy(source.at[e], target.at[e], large.at[e, i])
            for i, (source, target) in enumerate(((inv_hbm, inv), (val_hbm, val), (exp_hbm, exp)))
        ]
        for e in range(2)
    ]
    for copy in scalars + images[0] + images[1]:
        copy.start()
    for copy in scalars:
        copy.wait()
    rows = [row_map(off[0, 0, e, 0], sub[0, 0, e, 0]) for e in range(2)]
    cols = [col_map(off[0, 0, e, 1], sub[0, 0, e, 1]) for e in range(2)]
    halves = []
    for e in range(2):
        row_maps[e] = rows[e]
        col_maps[e, 0], col_maps[e, 1] = cols[e]
        for copy in images[e]:
            copy.wait()
        covered = cov[0, 0, e].astype(F32)
        masked = inv[e] * (val[e].astype(F32) * covered)
        data = jnp.concatenate([masked * exp[e], masked], axis=1).astype(BF16)
        middle[e] = data[96:224]
        halves.append(
            jnp.concatenate(
                [
                    dot(rows[e][low:high], jnp.concatenate([data[at : at + 128]] * 2, axis=0))
                    for at, low, high in ((0, 0, 112), (192, 16, 128))
                ],
                axis=0,
            ).astype(BF16)
        )
    odd = is_odd("dec")
    for n, whole in enumerate(warp_cols(halves, cols)):
        own[n, :80], own[n, 80:] = whole[32:112], whole[112:192]
        top, bottom = whole[:BAND], whole[128:]
        near[n] = jnp.where(odd, top, bottom).astype(BF16)
        far[n] = jnp.where(odd, bottom, top).astype(BF16)


def middle_kernel(middle, row_maps, col_maps, own):
    halves = [
        dot(row_maps[e, 16:112], jnp.concatenate([middle[e]] * 2, axis=0)).astype(BF16)
        for e in range(2)
    ]
    own[0], own[1] = warp_cols(halves, [(col_maps[e, 0], col_maps[e, 1]) for e in range(2)])


def dec_sum(own, mid, near, far, odd, n, block):
    cut = pl.ds(block * 128 if isinstance(block, int) else pl.multiple_of(block * 128, 128), 128)
    first, second = near[n, :, cut].astype(F32), far[n, :, cut].astype(F32)
    above, below = jnp.where(odd, first, second), jnp.where(odd, second, first)
    return jnp.concatenate(
        [
            own[n, :80, cut] + above[:80],
            mid[n, :16, cut] + above[80:],
            mid[n, 16:80, cut],
            mid[n, 80:, cut] + below[:16],
            own[n, 80:, cut] + below[16:],
        ],
        axis=0,
    )


def pack(planes):
    lane = lax.broadcasted_iota(jnp.int32, (128, 128), 1)
    groups = [plane[128 * i : 128 * i + 128] for plane in planes for i in range(2)]
    return jnp.concatenate(
        [
            jnp.where(lane < 96, groups[i], pltpu.roll(groups[3], 96 - 32 * i, 1))
            for i in range(3)
        ],
        axis=0,
    )


def unpack(packed):
    lane = lax.broadcasted_iota(jnp.int32, (128, 128), 1)
    groups = [packed[128 * i : 128 * i + 128] for i in range(3)]
    last = pltpu.roll(groups[0], 32, 1)
    last = jnp.where(lane < 32, last, pltpu.roll(groups[1], 64, 1))
    last = jnp.where(lane < 64, last, pltpu.roll(groups[2], 96, 1))
    groups.append(last)
    return [jnp.concatenate(groups[2 * n : 2 * n + 2], axis=0) for n in range(2)]


def edges_kernel(own, mid, near, far, one, two):
    odd = is_odd("dec")
    west = pack([dec_sum(own, mid, near, far, odd, n, 0) for n in range(2)])
    east = pack([pltpu.roll(dec_sum(own, mid, near, far, odd, n, 2), 96, 1) for n in range(2)])
    odd = is_odd("ra")
    one[...] = jnp.where(odd, west, east).astype(BF16)
    two[...] = jnp.where(odd, east, west).astype(BF16)


def psf_kernel(psf, weights, taps):
    down = lax.broadcasted_iota(jnp.int32, (SIDE, 128), 0)
    across = lax.broadcasted_iota(jnp.int32, (SIDE, 128), 1)
    reverse = jnp.where(((down + across) & 127) == 0, 1.0, 0.0).astype(BF16)
    taps[...] = jnp.zeros((80, 128), F32)
    taps[8 : 8 + SIDE] = dot(psf[...], reverse)
    lane = lax.broadcasted_iota(jnp.int32, (128, 128), 1)
    weights[0] = jnp.zeros((256, 128), BF16)
    weights[TILES_K] = jnp.zeros((256, 128), BF16)
    before = jnp.zeros((128, 128), F32)
    for q in range(64):
        here = jnp.broadcast_to(taps[8 + q : 9 + q], (128, 128))
        here = pltpu.roll(here, 0, 1, stride=1, stride_axis=0)
        prev = jnp.concatenate([before[64:], before[:64]], axis=0)
        weights[1 + q // 2, 128 * (q % 2) : 128 * (q % 2) + 128] = jnp.where(
            lane < 64, here, prev
        ).astype(BF16)
        before = here


def half_match(half, own, mid, near, far, bands, weights, weight, windows, stage):
    lane = lax.broadcasted_iota(jnp.int32, (EXT, 128), 1)
    east = half == 1
    odd = is_odd("dec")
    planes = []
    for n in range(2):
        band = unpack(bands)[n]
        band = jnp.where(
            east, jnp.where(lane < 96, band, 0.0), jnp.where(lane >= 32, pltpu.roll(band, 32, 1), 0.0)
        )
        left = dec_sum(own, mid, near, far, odd, n, half)
        right = dec_sum(own, mid, near, far, odd, n, half + 1)
        planes.append(
            jnp.concatenate(
                [left + jnp.where(east, 0.0, band), right + jnp.where(east, band, 0.0)], axis=1
            )
        )
    numer, denom = planes
    row = lax.broadcasted_iota(jnp.int32, (EXT, 256), 0) + (lax.axis_index("dec") * ROWS - 32)
    inside = (row >= 0) & (row < lax.axis_size("dec") * ROWS)
    coadd = jnp.where(inside, numer / jnp.maximum(denom, 1.0), 0.0).astype(BF16).astype(F32)
    weight(pltpu.roll(denom, 256 - 64, 1)[32 : 32 + ROWS, :128])
    for k in range(2):
        windows[k] = pltpu.roll(coadd, 256 - LEFT - 64 * k, 1)[:, :128]
    total = None
    for t in range(TILES_K):
        left = jnp.concatenate(
            [
                jnp.concatenate(
                    [windows[k, pl.ds(2 * t + s + 1, 48, stride=4), :] for k in range(2)], axis=0
                )
                for s in range(2)
            ],
            axis=1,
        ).astype(BF16)
        right = jnp.concatenate([weights[t + 1], weights[t]], axis=1)
        part = dot(left, right)
        total = part if total is None else total + part
    lane = lax.broadcasted_iota(jnp.int32, (48, 128), 1)
    for p in range(4):
        cut = slice(128 * (p // 2), 128 * (p // 2) + 128)
        low, high = total[:48, cut], total[48:, cut]
        if p % 2:
            low = pltpu.roll(low, 64, 1)
        else:
            high = pltpu.roll(high, 64, 1)
        stage[pl.ds(p, 48, stride=4), :] = jnp.where(lane < 64, low, high)


def first_kernel(own, mid, near, far, one, other, weights, out, weight_map, windows):
    def weight(value):
        weight_map[...] = value

    half = 1 - (lax.axis_index("ra") & 1)
    bands = one[...].astype(F32) + other[...].astype(F32)
    half_match(half, own, mid, near, far, bands, weights, weight, windows, out)


def second_kernel(
    own, mid, near, far, two, weights, ready, ready_weight,
    out, weight_map,
    windows, stage, stage_weight, sems,
):
    half = lax.axis_index("ra") & 1
    this, that = (pl.ds(pl.multiple_of(128 * x, 128), 128) for x in (half, 1 - half))
    copies = [
        pltpu.make_async_copy(source, target, sems.at[i])
        for i, (source, target) in enumerate(
            (
                (ready, out.at[:, that]),
                (ready_weight, weight_map.at[:, that]),
                (stage_weight, weight_map.at[:, this]),
                (stage, out.at[:, this]),
            )
        )
    ]
    copies[0].start()
    copies[1].start()

    def weight(value):
        stage_weight[...] = value
        copies[2].start()

    half_match(half, own, mid, near, far, two[...].astype(F32), weights, weight, windows, stage)
    copies[3].start()
    for copy in copies:
        copy.wait()


HBM = pl.BlockSpec(memory_space=pltpu.HBM)
VMEM = pl.BlockSpec(memory_space=pltpu.VMEM)


def call(body, ins, outs, scratch=(), flops=0, limit=16, space=None):
    return pl.pallas_call(
        body,
        in_specs=ins,
        out_specs=tuple(space or VMEM for _ in outs),
        out_shape=outs,
        scratch_shapes=scratch,
        cost_estimate=pl.CostEstimate(flops=flops, transcendentals=0, bytes_accessed=4_000_000),
        compiler_params=pltpu.CompilerParams(vmem_limit_bytes=limit * 1024 * 1024),
    )


def array(shape, kind):
    return jax.ShapeDtypeStruct(shape, kind)


def shards(exposures, inv_variance, pixel_valid, correlation, pixel_offset, subpixel, psf_match):
    own, near, far, middle, row_maps, col_maps = call(
        warp_kernel,
        [HBM] * 6,
        (
            array((2, 160, PCOLS), F32),
            array((2, BAND, PCOLS), BF16),
            array((2, BAND, PCOLS), BF16),
            array((2, 128, 2 * PCOLS), BF16),
            array((2, 128, 256), BF16),
            array((2, 2, 256, 256), BF16),
        ),
        scratch=[
            pltpu.SMEM((1, 1, 2, 2), jnp.int32),
            pltpu.SMEM((1, 1, 2, 2), F32),
            pltpu.SMEM((1, 1, 2), jnp.int32),
            pltpu.VMEM((2, PROWS, PCOLS), F32),
            pltpu.VMEM((2, PROWS, PCOLS), F32),
            pltpu.VMEM((2, PROWS, PCOLS), jnp.int32),
            pltpu.SemaphoreType.DMA((3,)),
            pltpu.SemaphoreType.DMA((2, 3)),
        ],
        flops=3_000_000_000,
    )(
        *(
            pltpu.with_memory_space_constraint(x, pltpu.HBM)
            for x in (pixel_offset, subpixel, correlation, exposures, inv_variance, pixel_valid)
        )
    )
    far = swap_pairs(far, "dec", lambda i: i % 2 == 1, False)
    near = swap_pairs(near, "dec", lambda i: i % 2 == 0, False)
    (weights,) = call(
        psf_kernel,
        [VMEM],
        (array((TILES_K + 1, 256, 128), BF16),),
        scratch=[pltpu.VMEM((80, 128), F32)],
        flops=3_000_000_000,
    )(psf_match)
    (mid,) = call(
        middle_kernel, [VMEM] * 3, (array((2, 96, PCOLS), F32),), flops=3_000_000_000
    )(middle, row_maps, col_maps)
    one, two = call(
        edges_kernel,
        [VMEM] * 4,
        (array((384, 128), BF16), array((384, 128), BF16)),
        flops=1_000_000,
    )(own, mid, near, far)
    first = swap_pairs(one, "ra", lambda i: i % 8 in (0, 2, 4), True)
    two = swap_pairs(two, "ra", lambda i: i % 2 == 1, True)
    last = swap_pairs(one, "ra", lambda i: i % 8 == 6, True)
    windows = pltpu.VMEM((2, EXT, 128), F32)
    stage = pltpu.VMEM((ROWS, 128), F32)
    ready, ready_weight = call(
        first_kernel,
        [VMEM] * 7,
        (array((ROWS, 128), F32), array((ROWS, 128), F32)),
        scratch=[windows],
        flops=3_000_000_000,
    )(own, mid, near, far, first, last, weights)
    return call(
        second_kernel,
        [VMEM] * 8,
        (array((ROWS, COLS), F32), array((ROWS, COLS), F32)),
        scratch=[windows, stage, stage, pltpu.SemaphoreType.DMA((4,))],
        flops=3_000_000_000,
        space=HBM,
    )(own, mid, near, far, two, weights, ready, ready_weight)


def solution(mesh):
    return jax.shard_map(
        shards,
        mesh=mesh,
        in_specs=(
            P(None, "dec", "ra"),
            P(None, "dec", "ra"),
            P(None, "dec", "ra"),
            P("dec", "ra", None),
            P("dec", "ra", None, None),
            P("dec", "ra", None, None),
            P(),
        ),
        out_specs=(P("dec", "ra"), P("dec", "ra")),
        check_vma=False,
    )
```

time: 36.6 us -> 37.1 us (1.014)
  starting transfers between devices: 22 us -> 22.7 us
  waiting for transfers between devices: 6.72 us -> 6.19 us
    pallas_call x3 -> x5, Pallas kernels: 5.7 us -> 6.5 us  [the longest x1 2.65 us: shards(): call(warp_kernel, [HBM] * 6, (array((2, 160, PCOLS), F32), array((2, BAND...]
    ppermute x4 -> x5, starting transfers between devices: 22 us -> 22.7 us  [swap_pairs(): return lax.ppermute(block, axis, pairs + [(b, a) for a, b in pairs])]
    pallas_call x1, Pallas kernels: 1.28 us -> 0.75 us  [shards(): call(psf_kernel, [VMEM], (array((TILES_K + 1, 256, 128), BF16),), scratch...]
    ppermute x4 -> x5, waiting for transfers between devices: 6.72 us -> 6.19 us  [swap_pairs(): return lax.ppermute(block, axis, pairs + [(b, a) for a, b in pairs])]
  transfers between devices with their start and end apart: 4 -> 5, of which waited for: 2 -> 2; matrix products, arithmetic and copies ran while one was open for 0% -> 0% of each run, Pallas kernels for 4% -> 7%
where the time goes in v1:
time: 37.1 us; the launch traced here: 36.9 us
  starting transfers between devices  22.7 us (61%)
  Pallas kernels  7.25 us (20%)
  waiting for transfers between devices  6.19 us (17%)
  between operations  0.75 us (2%)
    ppermute x5, starting transfers between devices, swap_pairs(): return lax.ppermute(block, axis, pairs + [(b, a) for a, b in pairs])  22.7 us
    ppermute x5, waiting for transfers between devices, swap_pairs(): return lax.ppermute(block, axis, pairs + [(b, a) for a, b in pairs])  6.19 us
    pallas_call x1, Pallas kernels, shards(): call(warp_kernel, [HBM] * 6, (array((2, 160, PCOLS), F32), array((2, BAND...  2.65 us
    pallas_call x1, Pallas kernels, shards(): call(second_kernel, [VMEM] * 8, (array((ROWS, COLS), F32), array((ROWS, C...  1.83 us
    pallas_call x1, Pallas kernels, shards(): call(first_kernel, [VMEM] * 7, (array((ROWS, 128), F32), array((ROWS, 128...  1.17 us
    pallas_call x1, Pallas kernels, shards(): call(psf_kernel, [VMEM], (array((TILES_K + 1, 256, 128), BF16),), scratch...  0.75 us
  transfers between devices with their start and end apart: 5, of which 2 were waited for; matrix products, arithmetic and copies ran while one was open for 0% of the time, Pallas kernels for 7%

profile of v1, /device:TPU:1, one launch (start us, length us, event | category | flops | bytes accessed | tf_op | source)
XLA Modules:
  0.0 36.9 jit_solution(16109372227379193298)
XLA Ops:
  0.6 2.6 %shard_map.86 = (f32[2,160,384]{2,1,0:T(8,128)S(1)}, bf16[2,96,384]{2,1,0:T(8,128)(2,1)S(1)}, bf16[2,96,384]{2,1,0:T(8,128)(2,1)S(1)}, bf16[2,128,768]{2,1,0:T(8...) custom-call(s32[1,1,2,2]{3,2,1,0:T(2,128)} %off_hbm.1, f32[1,1,2,2]{3,2,1,0:T(2,128)} %sub_hbm.1, ...), custom_call_target="tpu_custom_call" | custom-call | flops 3000000000 | bytes 4000000 | tf_op jit(solution)/shard_map/pallas_call | solution.py:353
  3.3 8.7 %collective-permute-start = (bf16[2,96,384]{2,1,0:T(8,128)(2,1)S(1)}, bf16[2,96,384]{2,1,0:T(8,128)(2,1)S(1)}, u32[]{:S(2)}, u32[]{:S(2)}) collective-permute-start(bf16[2,96,384]{2,1,0:T(8,128)(2,1)S(1)} %get-tuple-element.16), channel_id=1, source_target_pairs={{0,1},{2,3},{1,0},{3,2},{4,5},{6,7},{5,4},{7,6},{8,9},{10,11},{9,8... | collective-permute-start | bytes 442376 | tf_op jit(solution)/shard_map/ppermute | solution.py:30
  12.0 1.9 %collective-permute-start.1 = (bf16[2,96,384]{2,1,0:T(8,128)(2,1)S(1)}, bf16[2,96,384]{2,1,0:T(8,128)(2,1)S(1)}, u32[]{:S(2)}, u32[]{:S(2)}) collective-permute-start(bf16[2,96,384]{2,1,0:T(8,128)(2,1)S(1)} %get-tuple-element.17), channel_id=1, source_target_pairs={{1,2},{2,1},{5,6},{6,5},{9,10},{10,9},{13,14},{14,13},{17,18},{18,... | collective-permute-start | bytes 442376 | tf_op jit(solution)/shard_map/ppermute | solution.py:30
  14.0 0.0 copy-start
  14.0 0.6 %shard_map.87.mid = f32[2,96,384]{2,1,0:T(8,128)S(1)} custom-call(bf16[2,128,768]{2,1,0:T(8,128)(2,1)S(1)} %get-tuple-element.13.middle, bf16[2,128,256]{2,1,0:T(8,128)(2,1)S(1)} %get-tuple-element.14.row_maps, bf16[2,2,256,256]{3,2,1,0:T(8,128)(2,1)S(1)} %get-tuple-element.15.col_maps), custom_call_target="tpu_custom_call" | custom-call | flops 3000000000 | bytes 4000000 | tf_op jit(solution)/shard_map/pallas_call | solution.py:390
  14.6 0.0 collective-permute-done.near
  14.6 5.4 %collective-permute-done.1.far = bf16[2,96,384]{2,1,0:T(8,128)(2,1)S(1)} collective-permute-done((bf16[2,96,384]{2,1,0:T(8,128)(2,1)S(1)}, bf16[2,96,384]{2,1,0:T(8,128)(2,1)S(1)}, u32[]{:S(2)}, u32[]{:S(2)}) %collective-permute-start.1) | collective-permute-done | bytes 147488 | tf_op jit(solution)/shard_map/ppermute | solution.py:30
  20.0 0.2 shard_map.88
  20.3 0.7 %collective-permute-start.4 = (bf16[384,128]{1,0:T(8,128)(2,1)S(1)}, bf16[384,128]{1,0:T(8,128)(2,1)S(1)}, u32[]{:S(2)}, u32[]{:S(2)}) collective-permute-start(bf16[384,128]{1,0:T(8,128)(2,1)S(1)} %get-tuple-element.19), channel_id=1, source_target_pairs={{24,28},{56,60},{88,92},{120,124},{152,156},{184,188},{216,220},{2... | collective-permute-start | bytes 294920 | tf_op jit(solution)/shard_map/ppermute | solution.py:30
  20.9 1.9 %collective-permute-start.3 = (bf16[384,128]{1,0:T(8,128)(2,1)S(1)}, bf16[384,128]{1,0:T(8,128)(2,1)S(1)}, u32[]{:S(2)}, u32[]{:S(2)}) collective-permute-start(bf16[384,128]{1,0:T(8,128)(2,1)S(1)} %get-tuple-element.19), channel_id=1, source_target_pairs={{0,4},{8,12},{16,20},{32,36},{40,44},{48,52},{64,68},{72,76},{80,8... | collective-permute-start | bytes 294920 | tf_op jit(solution)/shard_map/ppermute | solution.py:30
  22.9 0.0 copy-done
  22.9 0.7 %shard_map.89.weights = bf16[34,256,128]{2,1,0:T(8,128)(2,1)S(1)} custom-call(bf16[63,63]{1,0:T(8,128)(2,1)S(1)} %copy-done), custom_call_target="tpu_custom_call" | custom-call | flops 3000000000 | bytes 4000000 | tf_op jit(solution)/shard_map/pallas_call | solution.py:383
  23.6 9.4 %collective-permute-start.2 = (bf16[384,128]{1,0:T(8,128)(2,1)S(1)}, bf16[384,128]{1,0:T(8,128)(2,1)S(1)}, u32[]{:S(2)}, u32[]{:S(2)}) collective-permute-start(bf16[384,128]{1,0:T(8,128)(2,1)S(1)} %get-tuple-element.18), channel_id=1, source_target_pairs={{4,8},{12,16},{20,24},{28,32},{36,40},{44,48},{52,56},{60,64},{68,... | collective-permute-start | bytes 294920 | tf_op jit(solution)/shard_map/ppermute | solution.py:30
  33.0 0.0 collective-permute-done.4.other
  33.1 0.0 collective-permute-done.3.one
  33.1 1.2 %shard_map.90 = (f32[192,128]{1,0:T(8,128)S(1)}, f32[192,128]{1,0:T(8,128)S(1)}) custom-call(f32[2,160,384]{2,1,0:T(8,128)S(1)} %get-tuple-element.12.own, f32[2,96,384]{2,1,0:T(8,128)S(1)} %shard_map.87.mid, bf16[2,96,384]{2,1,0:T(8,128)(2,1)S(1)} %collective-permute-done.near, bf16[2,96,384]{2,1,0:T(8,128)(2,1)S(1)} %collective-permute-done.1.far, ...), custom_call_target="tpu_custom_call" | custom-call | flops 3000000000 | bytes 4000000 | tf_op jit(solution)/shard_map/pallas_call | solution.py:404
  34.2 0.8 %collective-permute-done.2.two = bf16[384,128]{1,0:T(8,128)(2,1)S(1)} collective-permute-done((bf16[384,128]{1,0:T(8,128)(2,1)S(1)}, bf16[384,128]{1,0:T(8,128)(2,1)S(1)}, u32[]{:S(2)}, u32[]{:S(2)}) %collective-permute-start.2) | collective-permute-done | bytes 98336 | tf_op jit(solution)/shard_map/ppermute | solution.py:30
  35.0 1.8 %shard_map.91 = (f32[192,256]{1,0:T(8,128)}, f32[192,256]{1,0:T(8,128)}) custom-call(f32[2,160,384]{2,1,0:T(8,128)S(1)} %get-tuple-element.12.own, f32[2,96,384]{2,1,0:T(8,128)S(1)} %shard_map.87.mid, bf16[2,96,384]{2,1,0:T(8,128)(2,1)S(1)} %collective-permute-done.near, bf16[2,96,384]{2,1,0:T(8,128)(2,1)S(1)} %collective-permute-done.1.far, ...), custom_call_target="tpu_custom_call" | custom-call | flops 3000000000 | bytes 4000000 | tf_op jit(solution)/shard_map/pallas_call | solution.py:411
Async XLA Ops:
  3.3 11.3 %collective-permute-start = (bf16[2,96,384]{2,1,0:T(8,128)(2,1)S(1)}, bf16[2,96,384]{2,1,0:T(8,128)(2,1)S(1)}, u32[]{:S(2)}, u32[]{:S(2)}) collective-permute-start(bf16[2,96,384]{2,1,0:T(8,128)(2,1)S(1)} %get-tuple-element.16), channel_id=1, source_target_pairs={{0,1},{2,3},{1,0},{3,2},{4,5},{6,7},{5,4},{7,6},{8,9},{10,11},{9,8... | collective-permute-start | bytes 442376 | tf_op jit(solution)/shard_map/ppermute | solution.py:30
  12.0 8.0 %collective-permute-start.1 = (bf16[2,96,384]{2,1,0:T(8,128)(2,1)S(1)}, bf16[2,96,384]{2,1,0:T(8,128)(2,1)S(1)}, u32[]{:S(2)}, u32[]{:S(2)}) collective-permute-start(bf16[2,96,384]{2,1,0:T(8,128)(2,1)S(1)} %get-tuple-element.17), channel_id=1, source_target_pairs={{1,2},{2,1},{5,6},{6,5},{9,10},{10,9},{13,14},{14,13},{17,18},{18,... | collective-permute-start | bytes 442376 | tf_op jit(solution)/shard_map/ppermute | solution.py:30
  14.0 8.9 %copy-start = (bf16[63,63]{1,0:T(8,128)(2,1)S(1)}, bf16[63,63]{1,0:T(8,128)(2,1)}, u32[]{:S(2)}) copy-start(bf16[63,63]{1,0:T(8,128)(2,1)} %psf.1) | copy-start | bytes 23818
  20.3 12.8 %collective-permute-start.4 = (bf16[384,128]{1,0:T(8,128)(2,1)S(1)}, bf16[384,128]{1,0:T(8,128)(2,1)S(1)}, u32[]{:S(2)}, u32[]{:S(2)}) collective-permute-start(bf16[384,128]{1,0:T(8,128)(2,1)S(1)} %get-tuple-element.19), channel_id=1, source_target_pairs={{24,28},{56,60},{88,92},{120,124},{152,156},{184,188},{216,220},{2... | collective-permute-start | bytes 294920 | tf_op jit(solution)/shard_map/ppermute | solution.py:30
  20.9 12.1 %collective-permute-start.3 = (bf16[384,128]{1,0:T(8,128)(2,1)S(1)}, bf16[384,128]{1,0:T(8,128)(2,1)S(1)}, u32[]{:S(2)}, u32[]{:S(2)}) collective-permute-start(bf16[384,128]{1,0:T(8,128)(2,1)S(1)} %get-tuple-element.19), channel_id=1, source_target_pairs={{0,4},{8,12},{16,20},{32,36},{40,44},{48,52},{64,68},{72,76},{80,8... | collective-permute-start | bytes 294920 | tf_op jit(solution)/shard_map/ppermute | solution.py:30
  23.6 11.4 %collective-permute-start.2 = (bf16[384,128]{1,0:T(8,128)(2,1)S(1)}, bf16[384,128]{1,0:T(8,128)(2,1)S(1)}, u32[]{:S(2)}, u32[]{:S(2)}) collective-permute-start(bf16[384,128]{1,0:T(8,128)(2,1)S(1)} %get-tuple-element.18), channel_id=1, source_target_pairs={{4,8},{12,16},{20,24},{28,32},{36,40},{44,48},{52,56},{60,64},{68,... | collective-permute-start | bytes 294920 | tf_op jit(solution)/shard_map/ppermute | solution.py:30
